TPU v7x, 16 devices: a whole 2x2x2 slice. The times are simulated.
16 devices in a mesh: mp: 2 (over z), dp: 8 (over y, x, core).
Axes of the slice: x: 2, y: 2, z: 2, core: 2. Of those that a mesh axis runs over, the one named last changes fastest.
Arguments:
- a_mat: bfloat16 [4096, 65536], P(('mp', 'dp'))
- b_mat: bfloat16 [65536, 4096], P(('mp', 'dp'))
Outputs:
- output: bfloat16 [4096, 4096], P(('mp', 'dp'))
All inputs are finite; a program needn't handle non-finite values.
Results may differ from a plain program's by a relative error of at most 0.001.
Values are sent between devices in bfloat16 or wider.
A program may use at most 1 GiB of HBM per device.

v0:
```python
import jax
import jax.numpy as jnp
from jax import lax
from jax.sharding import PartitionSpec as P


def solution(mesh):
    mp_size = mesh.shape["mp"]
    dp_size = mesh.shape["dp"]

    def local_product(a_rows, b_rows):
        row_count = a_rows.shape[0]
        tok_piece = b_rows.shape[0]
        a_split = a_rows.reshape(row_count, mp_size, dp_size, tok_piece)
        a_cols = lax.all_to_all(a_split, "dp", 2, 0, tiled=True)
        a_cols = a_cols.reshape(row_count * dp_size, mp_size, tok_piece)
        b_group = lax.all_gather(b_rows, "mp", axis=0, tiled=False)
        part_sum = jnp.einsum("rit,itn->rn", a_cols, b_group, preferred_element_type=jnp.float32)
        row_sum = lax.psum_scatter(part_sum, "dp", scatter_dimension=0, tiled=True)
        return row_sum.astype(jnp.bfloat16)

    return jax.shard_map(
        local_product,
        mesh=mesh,
        in_specs=(P(("mp", "dp"), None), P(("mp", "dp"), None)),
        out_specs=P(("mp", "dp"), None),
        check_vma=False,
    )
```

profile of v0, /device:TPU:0, one launch (start us, length us, event | category | flops | bytes accessed | tf_op | source)
XLA Modules:
  0.0 1155.1 jit_solution(2713962677815934622)
XLA Ops:
  6.5 0.0 all-gather.3.cloned.1.call-start
  6.5 0.7 all-gather.3.cloned.1.call-update
  7.3 0.0 reduce-scatter.2.cloned.1.call-start
  7.3 43.9 %copy.5 = bf16[256,65536]{0,1:T(8,128)(2,1)} copy(bf16[256,65536]{1,0:T(8,128)(2,1)} %param.2) | data formatting | bytes 67108864 | tf_op args[0]
  51.2 40.4 %copy.6 = bf16[256,2,8,4096]{3,0,1,2:T(8,128)(2,1)} copy(bf16[256,2,8,4096]{0,3,2,1:T(8,128)(2,1)} %bitcast.11) | data formatting | bytes 67108864 | tf_op jit(solution)/shard_map/reshape | solution.py:14
  91.6 375.5 %all_to_all.15 = bf16[256,2,8,4096]{3,0,1,2:T(8,128)(2,1)} all-to-all(bf16[256,2,8,4096]{3,0,1,2:T(8,128)(2,1)} %copy.6), channel_id=1, replica_groups=mesh['mp'=2,'dp'=8] {'dp'}, dimensions={2} | all-to-all | bytes 67108864 | tf_op jit(solution)/shard_map/all_to_all | solution.py:15
  467.0 22.9 %copy.7 = bf16[8,256,2,1,4096]{4,1,0,2,3:T(8,128)(2,1)} copy(bf16[8,256,2,1,4096]{4,1,2,0,3:T(8,128)(2,1)} %bitcast.10) | data formatting | bytes 67108864 | tf_op jit(solution)/shard_map/all_to_all | solution.py:15
  489.9 285.9 %all-gather.3.cloned.1.call-done = bf16[8192,4096]{1,0:T(8,128)(2,1)} async-done(((bf16[4096,4096]{1,0:T(8,128)(2,1)}), bf16[8192,4096]{1,0:T(8,128)(2,1)}) %all-gather.3.cloned.1.call-update) | async-done | bytes 67108880 | tf_op jit(solution)/shard_map/all_gather | solution.py:17
  775.8 169.6 %convolution_bitcast_fusion = f32[2048,4096]{1,0:T(8,128)} fusion(bf16[2048,2,4096]{2,0,1:T(8,128)(2,1)} %bitcast.12, bf16[2,4096,4096]{2,1,0:T(8,128)(2,1)} %bitcast.4), kind=kOutput, calls=%fused_computation | convolution fusion | flops 137438953472 | bytes 134217728 | tf_op jit(solution)/shard_map/rit,itn->rn/dot_general | solution.py:18
  945.4 0.0 reduce-scatter.2.cloned.1.call-update
  945.4 199.1 %reduce-scatter.2.cloned.1.call-done = f32[256,4096]{1,0:T(8,128)} async-done(((f32[2048,4096]{1,0:T(8,128)}), f32[256,4096]{1,0:T(8,128)}) %reduce-scatter.2.cloned.1.call-update) | async-done | bytes 4194320 | tf_op jit(solution)/shard_map/reduce_scatter | solution.py:19
  1144.5 3.8 convert_element_type.3
Async XLA Ops:
  6.5 769.2 %all-gather.3.cloned.1.call-start = ((), (), s32[]{:S(2)}) async-start(), calls=%async_computation.3 | async-start | bytes 100663296 | tf_op jit(solution)/shard_map/all_gather | solution.py:17
  7.3 1137.2 %reduce-scatter.2.cloned.1.call-start = ((), (), s32[]{:S(2)}) async-start(), calls=%async_computation.2 | async-start | bytes 37748736 | tf_op jit(solution)/shard_map/reduce_scatter | solution.py:19
Sparse Core Ops, SparseCore 0:
  8.9 766.8 all-gather.2
  945.5 198.9 reduce-scatter.1
where the time goes:
time: 1160 us
  waiting for transfers between devices  486 us (42%)
  blocking collectives  375 us (32%)
  matrix products  170 us (15%)
  local copies, waits for them, and re-layouts  107 us (9%)
  between operations  13.4 us (1%)
    all_to_all x1, blocking collectives, local_product(): a_cols = lax.all_to_all(a_split, 'dp', 2, 0, tiled=True)  375 us
    all_gather x1, waiting for transfers between devices, local_product(): b_group = lax.all_gather(b_rows, 'mp', axis=0, tiled=False)  286 us
    reduce_scatter x1, waiting for transfers between devices, local_product(): row_sum = lax.psum_scatter(part_sum, 'dp', scatter_dimension=0, tiled=True)  199 us
    dot_general x1, matrix products, local_product(): jnp.einsum('rit,itn->rn', a_cols, b_group, preferred_element_type=jnp.flo...  170 us
    unnamed x1, local copies, waits for them, and re-layouts  43.9 us
    reshape x1, local copies, waits for them, and re-layouts, local_product(): a_split = a_rows.reshape(row_count, mp_size, dp_size, tok_piece)  40.4 us
  transfers between devices with their start and end apart: 2, of which 2 were waited for; matrix products, arithmetic and copies ran while one was open for 9% of the time, Pallas kernels for 0%

commit v1 on v0

v1 whole, which is shorter than its diff:
```python
import jax
import jax.numpy as jnp
from jax import lax
from jax.experimental import pallas as pl
from jax.experimental.pallas import tpu as pltpu
from jax.sharding import PartitionSpec as P

MESH = pl.DeviceIdType.MESH
CHIPS = 8
STEPS = 4
COLS = 512
TWO_HOP = ((3, 1, 2), (6, 2, 4), (5, 4, 1))


def flip(chip, axis):
    return chip + axis * (1 - 2 * ((chip // axis) % 2))


def across(chip, rel):
    for axis in (1, 2, 4):
        if rel & axis:
            chip = flip(chip, axis)
    return chip


def axes_of(unit):
    turns = [(unit + k) % 3 for k in range(3)]
    return [1 + turn + turn // 2 for turn in turns]


def wait_bytes(ref, sem):
    pltpu.make_async_copy(ref, ref, sem).wait()


def kernel(
    a_ref, b_ref,
    c_ref, a_in, a_via, b_in, part, part_in,
    a_vm, b_vm, prod, total, fetched, sum_in, last_in, c_vm,
    a_out_sem, a_in_sem, via_sem, b_sem, a_load, b_load, prod_sem,
    part_out_sem, part_in_sem, sum_out_sem, sum_in_sem, last_out_sem, last_in_sem,
    fetch_sem, c_sem,
):
    mp, dp = lax.axis_index("mp"), lax.axis_index("dp")
    chip, core = mp * 4 + dp // 2, dp % 2
    rows = a_ref.shape[0]
    depth, width = b_ref.shape
    span = 2 * depth
    step_rows = rows // STEPS
    blocks = width // COLS
    units = STEPS * blocks

    def device(chip_no, core_no):
        return (chip_no // 4, (chip_no % 4) * 2 + core_no)

    def send(src, dst, send_sem, recv_sem, chip_no, core_no=core):
        pltpu.make_async_remote_copy(
            src, dst, send_sem, recv_sem, device_id=device(chip_no, core_no), device_id_type=MESH
        ).start()

    def chunk(step):
        return pl.ds(pl.multiple_of(step * step_rows, step_rows), step_rows)

    def a_block(step, rel):
        first = pl.multiple_of(across(chip, rel) * span, span)
        return a_ref.at[chunk(step), pl.ds(first, span)]

    def send_first(step):
        send(a_block(step, 7), a_in.at[6, chunk(step)], a_out_sem.at[6], a_in_sem.at[step], across(chip, 7))
        for k, (rel, first, _) in enumerate(TWO_HOP):
            send(a_block(step, rel), a_via.at[k, chunk(step)], a_out_sem.at[k], via_sem.at[step, k], flip(chip, first))
        for k, rel in enumerate((1, 2, 4)):
            send(a_block(step, rel), a_in.at[rel - 1, chunk(step)], a_out_sem.at[3 + k], a_in_sem.at[step], flip(chip, rel))

    def forward(step):
        for k, (rel, _, second) in enumerate(TWO_HOP):
            block = a_via.at[k, chunk(step)]
            wait_bytes(block, via_sem.at[step, k])
            send(block, a_in.at[rel - 1, chunk(step)], a_out_sem.at[7 + k], a_in_sem.at[step], flip(chip, second))

    barrier = pltpu.get_barrier_semaphore()
    for rel in (1, 2, 4, 7):
        pl.semaphore_signal(barrier, inc=1, device_id=device(across(chip, rel), core), device_id_type=MESH)
    pl.semaphore_signal(barrier, inc=1, device_id=device(chip, 1 - core), device_id_type=MESH)
    pl.semaphore_wait(barrier, 5)

    send_first(0)
    send(b_ref, b_in, b_sem.at[0], b_sem.at[1], chip, 1 - core)
    send_first(1)
    for step in range(2):
        forward(step)
        send_first(step + 2)

    def b_copies(block, slot):
        cols = pl.ds(pl.multiple_of(block * COLS, COLS), COLS)
        own = pl.ds(pl.multiple_of(core * depth, depth), depth)
        other = pl.ds(pl.multiple_of((1 - core) * depth, depth), depth)
        return (
            pltpu.make_async_copy(b_ref.at[:, cols], b_vm.at[slot, own], b_load.at[slot]),
            pltpu.make_async_copy(b_in.at[:, cols], b_vm.at[slot, other], b_load.at[slot]),
        )

    wait_bytes(b_in, b_sem.at[1])
    for copy in b_copies(0, 0):
        copy.start()

    def rel_rows(rel):
        return pl.ds(pl.multiple_of(rel * step_rows, step_rows), step_rows)

    def send_parts(unit):
        first, second, third = axes_of(unit)
        slot = unit % 2
        pltpu.make_async_copy(prod.at[slot], part.at[unit], prod_sem.at[slot]).wait()
        for k in range(4):
            rel = first + second * (k // 2) + third * (k % 2)
            send(part.at[unit, rel_rows(rel)], part_in.at[unit, k], part_out_sem, part_in_sem.at[unit], flip(chip, first))

    def multiply(step, _):
        @pl.when((step >= 1) & (step + 1 < STEPS))
        def _():
            forward(step + 1)

        wait_bytes(a_in.at[:, chunk(step)], a_in_sem.at[step])
        pltpu.make_async_copy(a_block(step, 0), a_vm.at[rel_rows(0)], a_load).start()
        for rel in range(1, CHIPS):
            pltpu.make_async_copy(a_in.at[rel - 1, chunk(step)], a_vm.at[rel_rows(rel)], a_load).start()
        wait_bytes(a_vm, a_load)

        def one_unit(block, _):
            unit = step * blocks + block
            slot = unit % 2

            @pl.when(unit + 1 < units)
            def _():
                for copy in b_copies((block + 1) % blocks, 1 - slot):
                    copy.start()

            wait_bytes(b_vm.at[slot], b_load.at[slot])
            prod[slot] = jnp.dot(a_vm[...], b_vm[slot], preferred_element_type=jnp.float32)
            pltpu.make_async_copy(prod.at[slot], part.at[unit], prod_sem.at[slot]).start()

            @pl.when(unit >= 1)
            def _():
                send_parts(unit - 1)

            return 0

        return lax.fori_loop(0, blocks, one_unit, 0)

    lax.fori_loop(0, STEPS, multiply, 0)
    send_parts(units - 1)

    def fetch(unit):
        _, second, third = axes_of(unit)
        slot = unit % 2
        wait_bytes(part_in.at[unit], part_in_sem.at[unit])
        pltpu.make_async_copy(part_in.at[unit], fetched.at[slot, 0], fetch_sem.at[slot]).start()
        for k in range(4):
            rel = second * (k // 2) + third * (k % 2)
            pltpu.make_async_copy(
                part.at[unit, rel_rows(rel)], fetched.at[slot, 1, k], fetch_sem.at[slot]
            ).start()

    fetch(0)

    def add_first(unit, _):
        _, second, _ = axes_of(unit)
        slot = unit % 2

        @pl.when(unit + 1 < units)
        def _():
            fetch(unit + 1)

        wait_bytes(fetched.at[slot], fetch_sem.at[slot])
        total[unit] = fetched[slot, 0] + fetched[slot, 1]
        for k in range(2):
            send(total.at[unit, 2 + k], sum_in.at[unit, k], sum_out_sem, sum_in_sem.at[unit], flip(chip, second))
        return 0

    lax.fori_loop(0, units, add_first, 0)

    def add_second(unit, _):
        _, _, third = axes_of(unit)
        wait_bytes(sum_in.at[unit], sum_in_sem.at[unit])
        for k in (1, 0):
            total[unit, k] = total[unit, k] + sum_in[unit, k]
        send(total.at[unit, 1], last_in.at[unit], last_out_sem, last_in_sem.at[unit], flip(chip, third))
        return 0

    lax.fori_loop(0, units, add_second, 0)

    def add_last(unit, _):
        wait_bytes(last_in.at[unit], last_in_sem.at[unit])
        c_vm[unit] = (total[unit, 0] + last_in[unit]).astype(c_vm.dtype)
        cols = pl.ds(pl.multiple_of((unit % blocks) * COLS, COLS), COLS)
        pltpu.make_async_copy(c_vm.at[unit], c_ref.at[chunk(unit // blocks), cols], c_sem).start()
        return 0

    lax.fori_loop(0, units, add_last, 0)

    wait_bytes(c_vm, c_sem)
    for k in range(10):
        wait_bytes(a_in.at[0], a_out_sem.at[k])
    wait_bytes(b_ref, b_sem.at[0])
    wait_bytes(part_in, part_out_sem)
    wait_bytes(sum_in, sum_out_sem)
    wait_bytes(last_in, last_out_sem)


def local_product(a_rows, b_rows):
    rows, inner = a_rows.shape
    depth, width = b_rows.shape
    span = inner // CHIPS
    step_rows = rows // STEPS
    units = STEPS * (width // COLS)
    f32, bf16 = jnp.float32, a_rows.dtype
    tile = (step_rows, COLS)
    dma = pltpu.SemaphoreType.DMA
    outs = pl.pallas_call(
        kernel,
        out_shape=[
            jax.ShapeDtypeStruct((rows, width), bf16),
            jax.ShapeDtypeStruct((CHIPS - 1, rows, span), bf16),
            jax.ShapeDtypeStruct((len(TWO_HOP), rows, span), bf16),
            jax.ShapeDtypeStruct((depth, width), bf16),
            jax.ShapeDtypeStruct((units, CHIPS * step_rows, COLS), f32),
            jax.ShapeDtypeStruct((units, 4) + tile, f32),
        ],
        in_specs=[pl.BlockSpec(memory_space=pl.ANY)] * 2,
        out_specs=[pl.BlockSpec(memory_space=pl.ANY)] * 6,
        scratch_shapes=[
            pltpu.VMEM((CHIPS * step_rows, span), bf16),
            pltpu.VMEM((2, span, COLS), bf16),
            pltpu.VMEM((2, CHIPS * step_rows, COLS), f32),
            pltpu.VMEM((units, 4) + tile, f32),
            pltpu.VMEM((2, 2, 4) + tile, f32),
            pltpu.VMEM((units, 2) + tile, f32),
            pltpu.VMEM((units,) + tile, f32),
            pltpu.VMEM((units,) + tile, bf16),
            dma((10,)), dma((STEPS,)), dma((STEPS, len(TWO_HOP))), dma((2,)), dma, dma((2,)), dma((2,)),
            dma, dma((units,)), dma, dma((units,)), dma, dma((units,)),
            dma((2,)), dma,
        ],
        compiler_params=pltpu.CompilerParams(
            collective_id=0, has_side_effects=True, vmem_limit_bytes=67043328
        ),
    )(a_rows, b_rows)
    return outs[0]


def solution(mesh):
    return jax.shard_map(
        local_product,
        mesh=mesh,
        in_specs=(P(("mp", "dp"), None), P(("mp", "dp"), None)),
        out_specs=P(("mp", "dp"), None),
        check_vma=False,
    )
```

time: 1160 us -> 585 us (0.50)
  Pallas kernels: 0 us -> 581 us
  waiting for transfers between devices: 486 us -> 0 us
  blocking collectives: 375 us -> 0 us
  matrix products: 170 us -> 0 us
  local copies, waits for them, and re-layouts: 107 us -> 3.13 us
  between operations: 13.4 us -> 0.01 us
    pallas_call x0 -> x1, Pallas kernels: none -> 581 us  [local_product(): pl.pallas_call(kernel, out_shape=[jax.ShapeDtypeStruct((rows, width), bf1...]
    all_to_all x1 -> x0, blocking collectives: 375 us -> none  [local_product(): a_cols = lax.all_to_all(a_split, 'dp', 2, 0, tiled=True)]
    all_gather x1 -> x0, waiting for transfers between devices: 286 us -> none  [local_product(): b_group = lax.all_gather(b_rows, 'mp', axis=0, tiled=False)]
    reduce_scatter x1 -> x0, waiting for transfers between devices: 199 us -> none  [local_product(): row_sum = lax.psum_scatter(part_sum, 'dp', scatter_dimension=0, tiled=True)]
    dot_general x1 -> x0, matrix products: 170 us -> none  [local_product(): jnp.einsum('rit,itn->rn', a_cols, b_group, preferred_element_type=jnp.flo...]
    unnamed x1, local copies, waits for them, and re-layouts: 43.9 us -> 3.13 us
    reshape x1 -> x0, local copies, waits for them, and re-layouts: 40.4 us -> none  [local_product(): a_split = a_rows.reshape(row_count, mp_size, dp_size, tok_piece)]
    all_to_all x1 -> x0, local copies, waits for them, and re-layouts: 22.9 us -> none  [local_product(): a_cols = lax.all_to_all(a_split, 'dp', 2, 0, tiled=True)]
  transfers between devices with their start and end apart: 2 -> 0, of which waited for: 2 -> 0; matrix products, arithmetic and copies ran while one was open for 9% -> 0% of each run, Pallas kernels for 0% -> 0%
where the time goes in v1:
time: 585 us; the launch traced here: 584 us
  Pallas kernels  581 us (99%)
    pallas_call x1, Pallas kernels, local_product(): pl.pallas_call(kernel, out_shape=[jax.ShapeDtypeStruct((rows, width), bf1...  581 us

profile of v1, /device:TPU:0, one launch (start us, length us, event | category | flops | bytes accessed | tf_op | source)
XLA Modules:
  0.0 584.0 jit_solution(3651384965577507091)
XLA Ops:
  0.0 580.8 %shard_map.28 = (bf16[256,4096]{1,0:T(8,128)(2,1)}, bf16[7,256,8192]{2,1,0:T(8,128)(2,1)}, bf16[3,256,8192]{2,1,0:T(8,128)(2,1)}, bf16[4096,4096]{1,0:T(8,128)(2...) custom-call(bf16[256,65536]{1,0:T(8,128)(2,1)} %a_ref.1, bf16[4096,4096]{1,0:T(8,128)(2,1)} %b_ref.1), custom_call_target="tpu_custom_call" | custom-call | tf_op jit(solution)/shard_map/pallas_call | solution.py:218
  580.8 3.1 copy.4

commit v2 on v1

--- a/solution.py
+++ b/solution.py
@@ -25,7 +25,9 @@
 
 def axes_of(unit):
     turns = [(unit + k) % 3 for k in range(3)]
-    return [1 + turn + turn // 2 for turn in turns]
+    first, second, third = [1 + turn + turn // 2 for turn in turns]
+    swap = 1 // (unit + 1)
+    return first, second + swap * (third - second), third + swap * (second - third)
 
 
 def wait_bytes(ref, sem):
@@ -171,9 +173,11 @@
             fetch(unit + 1)
 
         wait_bytes(fetched.at[slot], fetch_sem.at[slot])
-        total[unit] = fetched[slot, 0] + fetched[slot, 1]
-        for k in range(2):
-            send(total.at[unit, 2 + k], sum_in.at[unit, k], sum_out_sem, sum_in_sem.at[unit], flip(chip, second))
+        for k in (2, 3):
+            total[unit, k] = fetched[slot, 0, k] + fetched[slot, 1, k]
+            send(total.at[unit, k], sum_in.at[unit, k - 2], sum_out_sem, sum_in_sem.at[unit], flip(chip, second))
+        for k in (0, 1):
+            total[unit, k] = fetched[slot, 0, k] + fetched[slot, 1, k]
         return 0
 
     lax.fori_loop(0, units, add_first, 0)
@@ -181,9 +185,9 @@
     def add_second(unit, _):
         _, _, third = axes_of(unit)
         wait_bytes(sum_in.at[unit], sum_in_sem.at[unit])
-        for k in (1, 0):
-            total[unit, k] = total[unit, k] + sum_in[unit, k]
+        total[unit, 1] = total[unit, 1] + sum_in[unit, 1]
         send(total.at[unit, 1], last_in.at[unit], last_out_sem, last_in_sem.at[unit], flip(chip, third))
+        total[unit, 0] = total[unit, 0] + sum_in[unit, 0]
         return 0
 
     lax.fori_loop(0, units, add_second, 0)

time: 585 us -> 582 us (level)
  no operation moved by 1% of the time
where the time goes in v2:
time: 582 us
  Pallas kernels  579 us (99%)
    pallas_call x1, Pallas kernels, local_product(): pl.pallas_call(kernel, out_shape=[jax.ShapeDtypeStruct((rows, width), bf1...  579 us

profile of v2, /device:TPU:0, one launch (start us, length us, event | category | flops | bytes accessed | tf_op | source)
XLA Modules:
  0.0 581.7 jit_solution(16945457259463565629)
XLA Ops:
  0.0 578.5 %shard_map.28 = (bf16[256,4096]{1,0:T(8,128)(2,1)}, bf16[7,256,8192]{2,1,0:T(8,128)(2,1)}, bf16[3,256,8192]{2,1,0:T(8,128)(2,1)}, bf16[4096,4096]{1,0:T(8,128)(2...) custom-call(bf16[256,65536]{1,0:T(8,128)(2,1)} %a_ref.1, bf16[4096,4096]{1,0:T(8,128)(2,1)} %b_ref.1), custom_call_target="tpu_custom_call" | custom-call | tf_op jit(solution)/shard_map/pallas_call | solution.py:222
  578.5 3.1 copy.4

commit v3 on v2

--- a/solution.py
+++ b/solution.py
@@ -168,14 +168,14 @@
         _, second, _ = axes_of(unit)
         slot = unit % 2
 
-        @pl.when(unit + 1 < units)
-        def _():
-            fetch(unit + 1)
-
         wait_bytes(fetched.at[slot], fetch_sem.at[slot])
         for k in (2, 3):
             total[unit, k] = fetched[slot, 0, k] + fetched[slot, 1, k]
             send(total.at[unit, k], sum_in.at[unit, k - 2], sum_out_sem, sum_in_sem.at[unit], flip(chip, second))
+        @pl.when(unit + 1 < units)
+        def _():
+            fetch(unit + 1)
+
         for k in (0, 1):
             total[unit, k] = fetched[slot, 0, k] + fetched[slot, 1, k]
         return 0

time: 582 us -> 583 us (level)
  no operation moved by 1% of the time
where the time goes in v3:
time: 583 us; the launch traced here: 582 us
  Pallas kernels  579 us (99%)
    pallas_call x1, Pallas kernels, local_product(): pl.pallas_call(kernel, out_shape=[jax.ShapeDtypeStruct((rows, width), bf1...  579 us

profile of v3, /device:TPU:0, one launch (start us, length us, event | category | flops | bytes accessed | tf_op | source)
XLA Modules:
  0.0 581.7 jit_solution(6599364071640275933)
XLA Ops:
  0.0 578.5 %shard_map.28 = (bf16[256,4096]{1,0:T(8,128)(2,1)}, bf16[7,256,8192]{2,1,0:T(8,128)(2,1)}, bf16[3,256,8192]{2,1,0:T(8,128)(2,1)}, bf16[4096,4096]{1,0:T(8,128)(2...) custom-call(bf16[256,65536]{1,0:T(8,128)(2,1)} %a_ref.1, bf16[4096,4096]{1,0:T(8,128)(2,1)} %b_ref.1), custom_call_target="tpu_custom_call" | custom-call | tf_op jit(solution)/shard_map/pallas_call | solution.py:222
  578.5 3.1 copy.4
